TPU v7x, 128 devices: a whole 4x4x4 slice. The times are simulated.
128 devices in a mesh: seq: 32 (over y, z, core), batch: 4 (over x).
Axes of the slice: x: 4, y: 4, z: 4, core: 2. Of those that a mesh axis runs over, the one named last changes fastest.
Arguments:
- queries: bfloat16 [4, 4096, 4096], P('batch', 'seq'), may hold values from -130 to 130
- keys: bfloat16 [4, 4096, 1024], P('batch', 'seq'), may hold values from -4 to 4
- values: bfloat16 [4, 4096, 1024], P('batch', 'seq'), may hold values from -4 to 4
- lengths: int32 [4], P('batch'), may hold values from 2048 to 4096
- block_pos: int32 [4, 32], P('batch'), may hold values from 0 to 31, each once within a row
- w_in: bfloat16 [6144, 1024], replicated, may hold values from -0.078125 to 0.078125
- b_in: float32 [1024], replicated, may hold values from -3 to 3
- output_weight: bfloat16 [1024, 8], replicated, may hold values from -0.1875 to 0.1875
- output_bias: float32 [8], replicated, may hold values from 1 to 2
Outputs:
- grad_w_in: float32 [6144, 1024], P(('seq', 'batch'))
- grad_b_in: float32 [1024], replicated
- output_weight_gradient: float32 [1024, 8], replicated
- output_bias_gradient: float32 [8], replicated
Inputs may be any that keep to these rules, and one draw needn't show every extreme that they name: Each row of block_pos names every block 0 to 31 once.
All inputs are finite; a program needn't handle non-finite values.
Results may differ from a plain program's by a relative error of at most 0.0017.
The roundings to bfloat16 on the way count: a program that leaves them out, or rounds other values in their place, can miss the bound.
Values may be sent and summed in bfloat16 or wider, within the bound.
No kernel may reach another device: no remote copies, remote signals or barrier semaphores. Data moves between devices by JAX's collectives and lax.ppermute only.
A program may use at most 128 MiB of HBM per device.

v0:
```python
import math
import jax
import jax.numpy as jnp
from jax import lax
from jax.sharding import PartitionSpec as P


def split_up(array, dim, size):
    before, after = (array.shape[:dim], array.shape[dim + 1 :])
    return jnp.moveaxis(array.reshape(*before, size, -1, *after), dim, 0)


def sent_and_summed(array, axis, dim):
    size = lax.axis_size(axis)
    tiles = lax.all_to_all(split_up(array, dim, size), axis, 0, 0, tiled=True)
    return jnp.sum(tiles, axis=0)


def in_one(arrays, axis):
    ends = [0]
    for a in arrays:
        ends.append(ends[-1] + a.size)
    so_far = lax.psum(jnp.concatenate([a.ravel() for a in arrays]), axis)
    return tuple((so_far[b:e].reshape(a.shape) for a, b, e in zip(arrays, ends, ends[1:])))


def on_device(queries, keys, values, lengths, block_pos, w_in, b_in, output_weight, output_bias):
    q_rows = queries[0]
    k_rows = keys[0]
    v_rows = values[0]
    rows = q_rows.shape[0]
    heads_kv = output_weight.shape[1]
    head_size = k_rows.shape[1] // heads_kv
    group_index = q_rows.shape[1] // k_rows.shape[1]
    scale = 1.0 / math.sqrt(head_size)
    every_key = lax.all_gather(k_rows, "seq", axis=0, tiled=True)
    total = every_key.shape[0]
    order = block_pos[0]
    offsets = jnp.arange(rows, dtype=jnp.int32)
    key_pos = (order[:, None] * rows + offsets[None, :]).reshape(-1)
    mine = lax.axis_index("seq")
    query_pos = lax.dynamic_index_in_dim(order, mine, 0, keepdims=False) * rows + offsets
    limit = lengths[0]
    allowed = (key_pos[None, :] <= query_pos[:, None]) & (key_pos < limit)[None, :]
    query_live = (query_pos < limit).astype(jnp.float32)

    def group_mass(index, sums):
        q_part = lax.dynamic_slice_in_dim(
            q_rows, index * group_index * head_size, group_index * head_size, 1
        )
        q_part = q_part.reshape(rows, group_index, head_size)
        k_part = lax.dynamic_slice_in_dim(every_key, index * head_size, head_size, 1)
        scores = (
            jnp.einsum("qhd,kd->hqk", q_part, k_part, preferred_element_type=jnp.float32) * scale
        )
        masked = jnp.where(allowed[None], scores, -1e30)
        top = jnp.max(masked, axis=2, keepdims=True)
        weights = jnp.where(allowed[None], jnp.exp(masked - top), 0.0)
        denom = jnp.sum(weights, axis=2, keepdims=True)
        share = weights / denom * query_live[None, :, None]
        column = jnp.sum(share, axis=(0, 1))
        return lax.dynamic_update_index_in_dim(sums, column, index, 0)

    partial_value = lax.fori_loop(
        0, heads_kv, group_mass, jnp.zeros((heads_kv, total), jnp.float32)
    )
    mass = sent_and_summed(partial_value, "seq", 1)
    labels = jnp.log1p(mass).T
    features = jnp.concatenate([q_rows, k_rows, v_rows], axis=1)
    pre = jnp.dot(features, w_in, preferred_element_type=jnp.float32) + b_in
    act = jax.nn.silu(pre).astype(jnp.bfloat16)
    pred = jnp.dot(act, output_weight, preferred_element_type=jnp.float32) + output_bias
    norm = 1.0 / math.sqrt(lax.axis_size("batch") * total)
    resid = ((pred - labels) * query_live[:, None] * norm).astype(jnp.bfloat16)
    back = lax.dot_general(
        resid, output_weight, (((1,), (1,)), ((), ())), preferred_element_type=jnp.float32
    )
    sig = jax.nn.sigmoid(pre)
    delta = (back * sig * (1.0 + pre * (1.0 - sig))).astype(jnp.bfloat16)
    out_term = lax.dot_general(
        act, resid, (((0,), (0,)), ((), ())), preferred_element_type=jnp.float32
    )
    grad_b_in, output_weight_gradient, output_bias_gradient = in_one(
        (
            jnp.sum(delta.astype(jnp.float32), axis=0),
            out_term,
            jnp.sum(resid.astype(jnp.float32), axis=0),
        ),
        ("seq", "batch"),
    )
    grad_w_in = lax.psum_scatter(
        lax.dot_general(
            features, delta, (((0,), (0,)), ((), ())), preferred_element_type=jnp.float32
        ),
        ("seq", "batch"),
        scatter_dimension=0,
        tiled=True,
    )
    return (grad_w_in, grad_b_in, output_weight_gradient, output_bias_gradient)


def solution(mesh):
    return jax.shard_map(
        on_device,
        mesh=mesh,
        in_specs=(
            P("batch", "seq", None),
            P("batch", "seq", None),
            P("batch", "seq", None),
            P("batch"),
            P("batch", None),
            P(),
            P(),
            P(),
            P(),
        ),
        out_specs=(P(("seq", "batch"), None), P(), P(), P()),
        check_vma=False,
    )
```

profile of v0, /device:TPU:0, one launch (start us, length us, event | category | flops | bytes accessed | tf_op | source)
XLA Modules:
  0.0 518.8 jit_solution(12301234503528148574)
XLA Ops:
  15.2 50.5 %all-gather.3.cloned.1.call-done = bf16[1,4096,1024]{2,1,0:T(8,128)(2,1)} async-done(((bf16[1,128,1024]{2,1,0:T(8,128)(2,1)}), bf16[1,4096,1024]{2,1,0:T(8,128)(2,1)}) %all-gather.3.cloned.1.call-update) | async-done | bytes 8388624 | tf_op jit(solution)/shard_map/all_gather | solution.py:36
  65.7 170.6 %while.16 = (s32[]{:T(128)}, f32[8,4096]{1,0:T(8,128)}, bf16[4096,1024]{1,0:T(8,128)(2,1)}, bf16[128,4096]{0,1:T(8,128)(2,1)S(1)}, s32[128]{0:T(128)S(1)}, /*ind...) while((s32[]{:T(128)}, f32[8,4096]{1,0:T(8,128)}, ...), condition=%wide.region_4.5_spmd.clone, body=%wide.region_0.4_spmd.clone.sunk | while | flops 1097869184 | bytes 22091528 | solution.py:64
  68.4 8.6 %fusion.72 = f32[4,128,4096]{1,2,0:T(8,128)} fusion(pred[128,4096]{0,1:T(8,128)(4,1)S(1)} %compare_and_fusion.2, bf16[128,4,128]{0,2,1:T(8,128)(2,1)S(1)} %bitcast.69, bf16[4096,1024]{1,0:T(8,128)(2,1)} %get-tuple-element.300, s32[]{:T(128)S(6)} %select_n.79), kind=kOutput, calls=%fused_computation.2.clone.1 | convolution fusion | flops 545268736 | bytes 10616836 | tf_op jit(solution)/shard_map/while/body/eval_jaxpr/div | solution.py:60
  77.0 8.4 %multiply_reduce_fusion.2 = f32[4096]{0:T(1024)S(1)} fusion(f32[4,128,4096]{1,2,0:T(8,128)} %fusion.72, f32[128]{0:T(128)S(1)} %compare_convert_fusion.3, pred[128,4096]{0,1:T(8,128)(4,1)S(1)} %compare_and_fusion.2, bf16[128,4,128]{0,2,1:T(8,128)(2,1)S(1)} %bitcast.70, bf16[4096,1024]{1,0:T(8,128)(2,1)} %get-tuple-element.300, s32[]{:T(128)S(6)} %select_n.79), kind=kOutput, calls=%fused_computation.5.clone.1 | convolution fusion | flops 551551488 | bytes 10633732 | tf_op jit(solution)/shard_map/while/body/eval_jaxpr/sub | solution.py:58
  89.7 8.6 %fusion.72 = f32[4,128,4096]{1,2,0:T(8,128)} fusion(pred[128,4096]{0,1:T(8,128)(4,1)S(1)} %compare_and_fusion.2, bf16[128,4,128]{0,2,1:T(8,128)(2,1)S(1)} %bitcast.69, bf16[4096,1024]{1,0:T(8,128)(2,1)} %get-tuple-element.300, s32[]{:T(128)S(6)} %select_n.79), kind=kOutput, calls=%fused_computation.2.clone.1 | convolution fusion | flops 545268736 | bytes 10616836 | tf_op jit(solution)/shard_map/while/body/eval_jaxpr/div | solution.py:60
  98.3 8.4 %multiply_reduce_fusion.2 = f32[4096]{0:T(1024)S(1)} fusion(f32[4,128,4096]{1,2,0:T(8,128)} %fusion.72, f32[128]{0:T(128)S(1)} %compare_convert_fusion.3, pred[128,4096]{0,1:T(8,128)(4,1)S(1)} %compare_and_fusion.2, bf16[128,4,128]{0,2,1:T(8,128)(2,1)S(1)} %bitcast.70, bf16[4096,1024]{1,0:T(8,128)(2,1)} %get-tuple-element.300, s32[]{:T(128)S(6)} %select_n.79), kind=kOutput, calls=%fused_computation.5.clone.1 | convolution fusion | flops 551551488 | bytes 10633732 | tf_op jit(solution)/shard_map/while/body/eval_jaxpr/sub | solution.py:58
  111.0 8.6 %fusion.72 = f32[4,128,4096]{1,2,0:T(8,128)} fusion(pred[128,4096]{0,1:T(8,128)(4,1)S(1)} %compare_and_fusion.2, bf16[128,4,128]{0,2,1:T(8,128)(2,1)S(1)} %bitcast.69, bf16[4096,1024]{1,0:T(8,128)(2,1)} %get-tuple-element.300, s32[]{:T(128)S(6)} %select_n.79), kind=kOutput, calls=%fused_computation.2.clone.1 | convolution fusion | flops 545268736 | bytes 10616836 | tf_op jit(solution)/shard_map/while/body/eval_jaxpr/div | solution.py:60
  119.6 8.4 %multiply_reduce_fusion.2 = f32[4096]{0:T(1024)S(1)} fusion(f32[4,128,4096]{1,2,0:T(8,128)} %fusion.72, f32[128]{0:T(128)S(1)} %compare_convert_fusion.3, pred[128,4096]{0,1:T(8,128)(4,1)S(1)} %compare_and_fusion.2, bf16[128,4,128]{0,2,1:T(8,128)(2,1)S(1)} %bitcast.70, bf16[4096,1024]{1,0:T(8,128)(2,1)} %get-tuple-element.300, s32[]{:T(128)S(6)} %select_n.79), kind=kOutput, calls=%fused_computation.5.clone.1 | convolution fusion | flops 551551488 | bytes 10633732 | tf_op jit(solution)/shard_map/while/body/eval_jaxpr/sub | solution.py:58
  132.4 8.6 %fusion.72 = f32[4,128,4096]{1,2,0:T(8,128)} fusion(pred[128,4096]{0,1:T(8,128)(4,1)S(1)} %compare_and_fusion.2, bf16[128,4,128]{0,2,1:T(8,128)(2,1)S(1)} %bitcast.69, bf16[4096,1024]{1,0:T(8,128)(2,1)} %get-tuple-element.300, s32[]{:T(128)S(6)} %select_n.79), kind=kOutput, calls=%fused_computation.2.clone.1 | convolution fusion | flops 545268736 | bytes 10616836 | tf_op jit(solution)/shard_map/while/body/eval_jaxpr/div | solution.py:60
  141.0 8.4 %multiply_reduce_fusion.2 = f32[4096]{0:T(1024)S(1)} fusion(f32[4,128,4096]{1,2,0:T(8,128)} %fusion.72, f32[128]{0:T(128)S(1)} %compare_convert_fusion.3, pred[128,4096]{0,1:T(8,128)(4,1)S(1)} %compare_and_fusion.2, bf16[128,4,128]{0,2,1:T(8,128)(2,1)S(1)} %bitcast.70, bf16[4096,1024]{1,0:T(8,128)(2,1)} %get-tuple-element.300, s32[]{:T(128)S(6)} %select_n.79), kind=kOutput, calls=%fused_computation.5.clone.1 | convolution fusion | flops 551551488 | bytes 10633732 | tf_op jit(solution)/shard_map/while/body/eval_jaxpr/sub | solution.py:58
  149.3 1.6 dynamic_update_slice.13
  153.7 8.6 %fusion.72 = f32[4,128,4096]{1,2,0:T(8,128)} fusion(pred[128,4096]{0,1:T(8,128)(4,1)S(1)} %compare_and_fusion.2, bf16[128,4,128]{0,2,1:T(8,128)(2,1)S(1)} %bitcast.69, bf16[4096,1024]{1,0:T(8,128)(2,1)} %get-tuple-element.300, s32[]{:T(128)S(6)} %select_n.79), kind=kOutput, calls=%fused_computation.2.clone.1 | convolution fusion | flops 545268736 | bytes 10616836 | tf_op jit(solution)/shard_map/while/body/eval_jaxpr/div | solution.py:60
  162.3 8.4 %multiply_reduce_fusion.2 = f32[4096]{0:T(1024)S(1)} fusion(f32[4,128,4096]{1,2,0:T(8,128)} %fusion.72, f32[128]{0:T(128)S(1)} %compare_convert_fusion.3, pred[128,4096]{0,1:T(8,128)(4,1)S(1)} %compare_and_fusion.2, bf16[128,4,128]{0,2,1:T(8,128)(2,1)S(1)} %bitcast.70, bf16[4096,1024]{1,0:T(8,128)(2,1)} %get-tuple-element.300, s32[]{:T(128)S(6)} %select_n.79), kind=kOutput, calls=%fused_computation.5.clone.1 | convolution fusion | flops 551551488 | bytes 10633732 | tf_op jit(solution)/shard_map/while/body/eval_jaxpr/sub | solution.py:58
  175.0 8.6 %fusion.72 = f32[4,128,4096]{1,2,0:T(8,128)} fusion(pred[128,4096]{0,1:T(8,128)(4,1)S(1)} %compare_and_fusion.2, bf16[128,4,128]{0,2,1:T(8,128)(2,1)S(1)} %bitcast.69, bf16[4096,1024]{1,0:T(8,128)(2,1)} %get-tuple-element.300, s32[]{:T(128)S(6)} %select_n.79), kind=kOutput, calls=%fused_computation.2.clone.1 | convolution fusion | flops 545268736 | bytes 10616836 | tf_op jit(solution)/shard_map/while/body/eval_jaxpr/div | solution.py:60
  183.6 8.4 %multiply_reduce_fusion.2 = f32[4096]{0:T(1024)S(1)} fusion(f32[4,128,4096]{1,2,0:T(8,128)} %fusion.72, f32[128]{0:T(128)S(1)} %compare_convert_fusion.3, pred[128,4096]{0,1:T(8,128)(4,1)S(1)} %compare_and_fusion.2, bf16[128,4,128]{0,2,1:T(8,128)(2,1)S(1)} %bitcast.70, bf16[4096,1024]{1,0:T(8,128)(2,1)} %get-tuple-element.300, s32[]{:T(128)S(6)} %select_n.79), kind=kOutput, calls=%fused_computation.5.clone.1 | convolution fusion | flops 551551488 | bytes 10633732 | tf_op jit(solution)/shard_map/while/body/eval_jaxpr/sub | solution.py:58
  196.3 8.6 %fusion.72 = f32[4,128,4096]{1,2,0:T(8,128)} fusion(pred[128,4096]{0,1:T(8,128)(4,1)S(1)} %compare_and_fusion.2, bf16[128,4,128]{0,2,1:T(8,128)(2,1)S(1)} %bitcast.69, bf16[4096,1024]{1,0:T(8,128)(2,1)} %get-tuple-element.300, s32[]{:T(128)S(6)} %select_n.79), kind=kOutput, calls=%fused_computation.2.clone.1 | convolution fusion | flops 545268736 | bytes 10616836 | tf_op jit(solution)/shard_map/while/body/eval_jaxpr/div | solution.py:60
  204.9 8.4 %multiply_reduce_fusion.2 = f32[4096]{0:T(1024)S(1)} fusion(f32[4,128,4096]{1,2,0:T(8,128)} %fusion.72, f32[128]{0:T(128)S(1)} %compare_convert_fusion.3, pred[128,4096]{0,1:T(8,128)(4,1)S(1)} %compare_and_fusion.2, bf16[128,4,128]{0,2,1:T(8,128)(2,1)S(1)} %bitcast.70, bf16[4096,1024]{1,0:T(8,128)(2,1)} %get-tuple-element.300, s32[]{:T(128)S(6)} %select_n.79), kind=kOutput, calls=%fused_computation.5.clone.1 | convolution fusion | flops 551551488 | bytes 10633732 | tf_op jit(solution)/shard_map/while/body/eval_jaxpr/sub | solution.py:58
  217.6 8.6 %fusion.72 = f32[4,128,4096]{1,2,0:T(8,128)} fusion(pred[128,4096]{0,1:T(8,128)(4,1)S(1)} %compare_and_fusion.2, bf16[128,4,128]{0,2,1:T(8,128)(2,1)S(1)} %bitcast.69, bf16[4096,1024]{1,0:T(8,128)(2,1)} %get-tuple-element.300, s32[]{:T(128)S(6)} %select_n.79), kind=kOutput, calls=%fused_computation.2.clone.1 | convolution fusion | flops 545268736 | bytes 10616836 | tf_op jit(solution)/shard_map/while/body/eval_jaxpr/div | solution.py:60
  226.2 8.4 %multiply_reduce_fusion.2 = f32[4096]{0:T(1024)S(1)} fusion(f32[4,128,4096]{1,2,0:T(8,128)} %fusion.72, f32[128]{0:T(128)S(1)} %compare_convert_fusion.3, pred[128,4096]{0,1:T(8,128)(4,1)S(1)} %compare_and_fusion.2, bf16[128,4,128]{0,2,1:T(8,128)(2,1)S(1)} %bitcast.70, bf16[4096,1024]{1,0:T(8,128)(2,1)} %get-tuple-element.300, s32[]{:T(128)S(6)} %select_n.79), kind=kOutput, calls=%fused_computation.5.clone.1 | convolution fusion | flops 551551488 | bytes 10633732 | tf_op jit(solution)/shard_map/while/body/eval_jaxpr/sub | solution.py:58
  236.2 5.5 %all-to-all-start = ((f32[32,8,128]{2,1,0:T(8,128)}), f32[32,8,128]{2,1,0:T(8,128)S(1)}, u32[]{:S(2)}, u32[]{:S(2)}) async-start(f32[32,8,128]{2,1,0:T(8,128)} %bitcast.9), calls=%async_computation | async-start | bytes 262144 | tf_op jit(solution)/shard_map/all_to_all | solution.py:15
  242.0 6.5 %multiply_convert_fusion = (bf16[128,1024]{1,0:T(8,128)(2,1)S(1)}, f32[128,1024]{1,0:T(8,128)S(1)}) fusion(f32[1024]{0:T(1024)S(1)} %copy-done.1, bf16[6144,1024]{1,0:T(8,128)(2,1)} %param.16, bf16[128,1024]{0,1:T(8,128)(2,1)S(1)} %bitcast.73, bf16[128,1024]{0,1:T(8,128)(2,1)S(1)} %bitcast.71, bf16[128,4096]{0,1:T(8,128)(2,1)S(1)} %get-tuple-element.317), kind=kOutput, calls=%fused_computation.42 | convolution fusion | flops 1616117760 | bytes 14946304 | tf_op jit(solution)/shard_map/dot_general | solution.py:70
  250.3 13.2 %fusion.46 = f32[6144,1024]{1,0:T(8,128)} fusion(bf16[128,1024]{1,0:T(8,128)(2,1)S(1)} %get-tuple-element.212, bf16[128,1024]{0,1:T(8,128)(2,1)S(1)} %bitcast.74, bf16[128,1024]{0,1:T(8,128)(2,1)S(1)} %bitcast.72, bf16[128,4096]{0,1:T(8,128)(2,1)S(1)} %get-tuple-element.317), kind=kOutput, calls=%fused_computation.40 | convolution fusion | flops 1615331328 | bytes 27000832 | tf_op jit(solution)/shard_map/dot_general | solution.py:92
  264.1 67.0 %psum.7 = f32[9224]{0:T(1024)S(1)} all-reduce(f32[9224]{0:T(1024)S(1)} %pad_maximum_fusion.3), channel_id=1, replica_groups=mesh['seq'=32,'batch'=4] {'seq','batch'}, use_global_device_ids=true, to_apply=%region_9.10 | all-reduce | flops 9224 | bytes 73792 | tf_op jit(solution)/shard_map/psum | solution.py:23
  333.2 178.8 %reduce-scatter.2.cloned.1.call-done = f32[48,1024]{1,0:T(8,128)} async-done(((f32[6144,1024]{1,0:T(8,128)}), f32[48,1024]{1,0:T(8,128)}) %reduce-scatter.2.cloned.1.call-update) | async-done | bytes 196624 | tf_op jit(solution)/shard_map/reduce_scatter | solution.py:91
  (63 shorter events, 45.0 us)
Async XLA Ops:
  7.2 242.5 %copy-start = (bf16[1024,8]{0,1:T(8,128)(2,1)S(1)}, bf16[1024,8]{0,1:T(8,128)(2,1)}, u32[]{:S(2)}) copy-start(bf16[1024,8]{0,1:T(8,128)(2,1)} %param.18) | copy-start | bytes 49156
  7.2 58.5 %all-gather.3.cloned.1.call-start = ((), (), s32[]{:S(2)}) async-start(), calls=%async_computation.3 | async-start | bytes 8650752 | tf_op jit(solution)/shard_map/all_gather | solution.py:36
  65.7 176.3 %copy-start.1 = (f32[1024]{0:T(1024)S(1)}, f32[1024]{0:T(1024)}, u32[]{:S(2)}) copy-start(f32[1024]{0:T(1024)} %param.17) | copy-start | bytes 12292
  236.2 13.3 %all-to-all-start = ((f32[32,8,128]{2,1,0:T(8,128)}), f32[32,8,128]{2,1,0:T(8,128)S(1)}, u32[]{:S(2)}, u32[]{:S(2)}) async-start(f32[32,8,128]{2,1,0:T(8,128)} %bitcast.9), calls=%async_computation | async-start | bytes 262144 | tf_op jit(solution)/shard_map/all_to_all | solution.py:15
  241.7 270.2 %reduce-scatter.2.cloned.1.call-start = ((), (), s32[]{:S(2)}) async-start(), calls=%async_computation.2 | async-start | bytes 25362432 | tf_op jit(solution)/shard_map/reduce_scatter | solution.py:91
  242.0 7.6 %copy-start.2 = (f32[8]{0:T(128)S(1)}, f32[8]{0:T(128)}, u32[]{:S(2)}) copy-start(f32[8]{0:T(128)} %param.19) | copy-start | bytes 100
Sparse Core Ops, SparseCore 0:
  10.3 55.3 all-gather.2
  263.7 248.2 reduce-scatter.1
where the time goes:
time: 520 us; the launch traced here: 519 us
  waiting for transfers between devices  230 us (44%)
  matrix products  156 us (30%)
  blocking collectives  67 us (13%)
  other arithmetic  24.9 us (5%)
  local copies, waits for them, and re-layouts  19.4 us (4%)
  between operations  14.8 us (3%)
  starting transfers between devices  5.76 us (1%)
    reduce_scatter x1, waiting for transfers between devices, on_device(): lax.psum_scatter(lax.dot_general(features, delta, (((0,), (0,)), ((), ())...  179 us
    div x8, matrix products, group_mass(): share = weights / denom * query_live[None, :, None]  68.8 us
    sub x8, matrix products, group_mass(): weights = jnp.where(allowed[None], jnp.exp(masked - top), 0.0)  67 us
    psum x1, blocking collectives, in_one(): so_far = lax.psum(jnp.concatenate([a.ravel() for a in arrays]), axis)  67 us
    all_gather x1, waiting for transfers between devices, on_device(): every_key = lax.all_gather(k_rows, 'seq', axis=0, tiled=True)  50.5 us
    dot_general x1, matrix products, on_device(): lax.dot_general(features, delta, (((0,), (0,)), ((), ())), preferred_elem...  13.2 us
    dynamic_update_slice x8, local copies, waits for them, and re-layouts, group_mass(): return lax.dynamic_update_index_in_dim(sums, column, index, 0)  12.9 us
    and x8, other arithmetic, on_device(): (key_pos[None, :] <= query_pos[:, None]) & (key_pos < limit)[None, :]  11.1 us
  transfers between devices with their start and end apart: 3, of which 3 were waited for; matrix products, arithmetic and copies ran while one was open for 3% of the time, Pallas kernels for 0%

commit v1 on v0

--- a/solution.py
+++ b/solution.py
@@ -33,7 +33,8 @@
     head_size = k_rows.shape[1] // heads_kv
     group_index = q_rows.shape[1] // k_rows.shape[1]
     scale = 1.0 / math.sqrt(head_size)
-    every_key = lax.all_gather(k_rows, "seq", axis=0, tiled=True)
+    sent = jnp.stack([k_rows] * lax.axis_size("seq"))
+    every_key = jnp.concatenate(lax.all_to_all(sent, "seq", 0, 0), axis=0)
     total = every_key.shape[0]
     order = block_pos[0]
     offsets = jnp.arange(rows, dtype=jnp.int32)

time: 520 us -> 598 us (1.15)
  waiting for transfers between devices: 230 us -> 290 us
  starting transfers between devices: 5.76 us -> 23 us
    all_to_all x0 -> x1, waiting for transfers between devices: none -> 110 us  [on_device(): every_key = jnp.concatenate(lax.all_to_all(sent, 'seq', 0, 0), axis=0)]
    all_gather x1 -> x0, waiting for transfers between devices: 50.5 us -> none  [on_device(): every_key = lax.all_gather(k_rows, 'seq', axis=0, tiled=True)]
    all_to_all x0 -> x1, starting transfers between devices: none -> 8.72 us  [on_device(): every_key = jnp.concatenate(lax.all_to_all(sent, 'seq', 0, 0), axis=0)]
    all_to_all x1, starting transfers between devices: 5.5 us -> 14 us  [sent_and_summed(): tiles = lax.all_to_all(split_up(array, dim, size), axis, 0, 0, tiled=True)]
  transfers between devices with their start and end apart: 3 -> 3, of which waited for: 3 -> 3; matrix products, arithmetic and copies ran while one was open for 3% -> 2% of each run, Pallas kernels for 0% -> 0%
where the time goes in v1:
time: 598 us; the launch traced here: 597 us
  waiting for transfers between devices  290 us (48%)
  matrix products  156 us (26%)
  blocking collectives  67 us (11%)
  other arithmetic  23.6 us (4%)
  starting transfers between devices  23 us (4%)
  local copies, waits for them, and re-layouts  21.8 us (4%)
  between operations  14.9 us (2%)
    reduce_scatter x1, waiting for transfers between devices, on_device(): lax.psum_scatter(lax.dot_general(features, delta, (((0,), (0,)), ((), ())...  179 us
    all_to_all x1, waiting for transfers between devices, on_device(): every_key = jnp.concatenate(lax.all_to_all(sent, 'seq', 0, 0), axis=0)  110 us
    div x8, matrix products, group_mass(): share = weights / denom * query_live[None, :, None]  68.8 us
    psum x1, blocking collectives, in_one(): so_far = lax.psum(jnp.concatenate([a.ravel() for a in arrays]), axis)  67 us
    sub x8, matrix products, group_mass(): weights = jnp.where(allowed[None], jnp.exp(masked - top), 0.0)  67 us
    all_to_all x1, starting transfers between devices, sent_and_summed(): tiles = lax.all_to_all(split_up(array, dim, size), axis, 0, 0, tiled=True)  14 us
    dot_general x1, matrix products, on_device(): lax.dot_general(features, delta, (((0,), (0,)), ((), ())), preferred_elem...  13.2 us
    dynamic_update_slice x8, local copies, waits for them, and re-layouts, group_mass(): return lax.dynamic_update_index_in_dim(sums, column, index, 0)  12.9 us
  transfers between devices with their start and end apart: 3, of which 3 were waited for; matrix products, arithmetic and copies ran while one was open for 2% of the time, Pallas kernels for 0%

profile of v1, /device:TPU:0, one launch (start us, length us, event | category | flops | bytes accessed | tf_op | source)
XLA Modules:
  0.0 596.5 jit_solution(11090086855176707046)
XLA Ops:
  12.4 8.7 %all-to-all-start = ((bf16[32,128,1024]{2,1,0:T(8,128)(2,1)}), bf16[32,128,1024]{2,1,0:T(8,128)(2,1)}, u32[]{:S(2)}, u32[]{:S(2)}) async-start(bf16[32,128,1024]{2,1,0:T(8,128)(2,1)} %stack.3), calls=%async_computation | async-start | bytes 16777216 | tf_op jit(solution)/shard_map/all_to_all | solution.py:37
  24.3 110.4 %all-to-all-done = bf16[32,128,1024]{2,1,0:T(8,128)(2,1)} async-done(((bf16[32,128,1024]{2,1,0:T(8,128)(2,1)}), bf16[32,128,1024]{2,1,0:T(8,128)(2,1)}, u32[]{:S(2)}, u32[]{:S(2)}) %all-to-all-start) | async-done | bytes 8388640 | tf_op jit(solution)/shard_map/all_to_all | solution.py:37
  134.7 170.6 %while.16 = (s32[]{:T(128)}, f32[8,4096]{1,0:T(8,128)}, bf16[4096,1024]{1,0:T(8,128)(2,1)}, bf16[128,4096]{0,1:T(8,128)(2,1)S(1)}, s32[128]{0:T(128)S(1)}, /*ind...) while((s32[]{:T(128)}, f32[8,4096]{1,0:T(8,128)}, ...), condition=%wide.region_4.5_spmd.clone, body=%wide.region_0.4_spmd.clone.sunk | while | flops 1097869184 | bytes 22091528 | solution.py:65
  137.4 8.6 %fusion.72 = f32[4,128,4096]{1,2,0:T(8,128)} fusion(pred[128,4096]{0,1:T(8,128)(4,1)S(1)} %compare_and_fusion.2, bf16[128,4,128]{0,2,1:T(8,128)(2,1)S(1)} %bitcast.70, bf16[4096,1024]{1,0:T(8,128)(2,1)} %get-tuple-element.300, s32[]{:T(128)S(6)} %select_n.79), kind=kOutput, calls=%fused_computation.2.clone.1 | convolution fusion | flops 545268736 | bytes 10616836 | tf_op jit(solution)/shard_map/while/body/eval_jaxpr/div | solution.py:61
  146.0 8.4 %multiply_reduce_fusion.2 = f32[4096]{0:T(1024)S(1)} fusion(f32[4,128,4096]{1,2,0:T(8,128)} %fusion.72, f32[128]{0:T(128)S(1)} %compare_convert_fusion.3, pred[128,4096]{0,1:T(8,128)(4,1)S(1)} %compare_and_fusion.2, bf16[128,4,128]{0,2,1:T(8,128)(2,1)S(1)} %bitcast.71, bf16[4096,1024]{1,0:T(8,128)(2,1)} %get-tuple-element.300, s32[]{:T(128)S(6)} %select_n.79), kind=kOutput, calls=%fused_computation.5.clone.1 | convolution fusion | flops 551551488 | bytes 10633732 | tf_op jit(solution)/shard_map/while/body/eval_jaxpr/sub | solution.py:59
  158.7 8.6 %fusion.72 = f32[4,128,4096]{1,2,0:T(8,128)} fusion(pred[128,4096]{0,1:T(8,128)(4,1)S(1)} %compare_and_fusion.2, bf16[128,4,128]{0,2,1:T(8,128)(2,1)S(1)} %bitcast.70, bf16[4096,1024]{1,0:T(8,128)(2,1)} %get-tuple-element.300, s32[]{:T(128)S(6)} %select_n.79), kind=kOutput, calls=%fused_computation.2.clone.1 | convolution fusion | flops 545268736 | bytes 10616836 | tf_op jit(solution)/shard_map/while/body/eval_jaxpr/div | solution.py:61
  167.3 8.4 %multiply_reduce_fusion.2 = f32[4096]{0:T(1024)S(1)} fusion(f32[4,128,4096]{1,2,0:T(8,128)} %fusion.72, f32[128]{0:T(128)S(1)} %compare_convert_fusion.3, pred[128,4096]{0,1:T(8,128)(4,1)S(1)} %compare_and_fusion.2, bf16[128,4,128]{0,2,1:T(8,128)(2,1)S(1)} %bitcast.71, bf16[4096,1024]{1,0:T(8,128)(2,1)} %get-tuple-element.300, s32[]{:T(128)S(6)} %select_n.79), kind=kOutput, calls=%fused_computation.5.clone.1 | convolution fusion | flops 551551488 | bytes 10633732 | tf_op jit(solution)/shard_map/while/body/eval_jaxpr/sub | solution.py:59
  180.1 8.6 %fusion.72 = f32[4,128,4096]{1,2,0:T(8,128)} fusion(pred[128,4096]{0,1:T(8,128)(4,1)S(1)} %compare_and_fusion.2, bf16[128,4,128]{0,2,1:T(8,128)(2,1)S(1)} %bitcast.70, bf16[4096,1024]{1,0:T(8,128)(2,1)} %get-tuple-element.300, s32[]{:T(128)S(6)} %select_n.79), kind=kOutput, calls=%fused_computation.2.clone.1 | convolution fusion | flops 545268736 | bytes 10616836 | tf_op jit(solution)/shard_map/while/body/eval_jaxpr/div | solution.py:61
  188.7 8.4 %multiply_reduce_fusion.2 = f32[4096]{0:T(1024)S(1)} fusion(f32[4,128,4096]{1,2,0:T(8,128)} %fusion.72, f32[128]{0:T(128)S(1)} %compare_convert_fusion.3, pred[128,4096]{0,1:T(8,128)(4,1)S(1)} %compare_and_fusion.2, bf16[128,4,128]{0,2,1:T(8,128)(2,1)S(1)} %bitcast.71, bf16[4096,1024]{1,0:T(8,128)(2,1)} %get-tuple-element.300, s32[]{:T(128)S(6)} %select_n.79), kind=kOutput, calls=%fused_computation.5.clone.1 | convolution fusion | flops 551551488 | bytes 10633732 | tf_op jit(solution)/shard_map/while/body/eval_jaxpr/sub | solution.py:59
  201.4 8.6 %fusion.72 = f32[4,128,4096]{1,2,0:T(8,128)} fusion(pred[128,4096]{0,1:T(8,128)(4,1)S(1)} %compare_and_fusion.2, bf16[128,4,128]{0,2,1:T(8,128)(2,1)S(1)} %bitcast.70, bf16[4096,1024]{1,0:T(8,128)(2,1)} %get-tuple-element.300, s32[]{:T(128)S(6)} %select_n.79), kind=kOutput, calls=%fused_computation.2.clone.1 | convolution fusion | flops 545268736 | bytes 10616836 | tf_op jit(solution)/shard_map/while/body/eval_jaxpr/div | solution.py:61
  210.0 8.4 %multiply_reduce_fusion.2 = f32[4096]{0:T(1024)S(1)} fusion(f32[4,128,4096]{1,2,0:T(8,128)} %fusion.72, f32[128]{0:T(128)S(1)} %compare_convert_fusion.3, pred[128,4096]{0,1:T(8,128)(4,1)S(1)} %compare_and_fusion.2, bf16[128,4,128]{0,2,1:T(8,128)(2,1)S(1)} %bitcast.71, bf16[4096,1024]{1,0:T(8,128)(2,1)} %get-tuple-element.300, s32[]{:T(128)S(6)} %select_n.79), kind=kOutput, calls=%fused_computation.5.clone.1 | convolution fusion | flops 551551488 | bytes 10633732 | tf_op jit(solution)/shard_map/while/body/eval_jaxpr/sub | solution.py:59
  222.7 8.6 %fusion.72 = f32[4,128,4096]{1,2,0:T(8,128)} fusion(pred[128,4096]{0,1:T(8,128)(4,1)S(1)} %compare_and_fusion.2, bf16[128,4,128]{0,2,1:T(8,128)(2,1)S(1)} %bitcast.70, bf16[4096,1024]{1,0:T(8,128)(2,1)} %get-tuple-element.300, s32[]{:T(128)S(6)} %select_n.79), kind=kOutput, calls=%fused_computation.2.clone.1 | convolution fusion | flops 545268736 | bytes 10616836 | tf_op jit(solution)/shard_map/while/body/eval_jaxpr/div | solution.py:61
  231.3 8.4 %multiply_reduce_fusion.2 = f32[4096]{0:T(1024)S(1)} fusion(f32[4,128,4096]{1,2,0:T(8,128)} %fusion.72, f32[128]{0:T(128)S(1)} %compare_convert_fusion.3, pred[128,4096]{0,1:T(8,128)(4,1)S(1)} %compare_and_fusion.2, bf16[128,4,128]{0,2,1:T(8,128)(2,1)S(1)} %bitcast.71, bf16[4096,1024]{1,0:T(8,128)(2,1)} %get-tuple-element.300, s32[]{:T(128)S(6)} %select_n.79), kind=kOutput, calls=%fused_computation.5.clone.1 | convolution fusion | flops 551551488 | bytes 10633732 | tf_op jit(solution)/shard_map/while/body/eval_jaxpr/sub | solution.py:59
  244.0 8.6 %fusion.72 = f32[4,128,4096]{1,2,0:T(8,128)} fusion(pred[128,4096]{0,1:T(8,128)(4,1)S(1)} %compare_and_fusion.2, bf16[128,4,128]{0,2,1:T(8,128)(2,1)S(1)} %bitcast.70, bf16[4096,1024]{1,0:T(8,128)(2,1)} %get-tuple-element.300, s32[]{:T(128)S(6)} %select_n.79), kind=kOutput, calls=%fused_computation.2.clone.1 | convolution fusion | flops 545268736 | bytes 10616836 | tf_op jit(solution)/shard_map/while/body/eval_jaxpr/div | solution.py:61
  252.6 8.4 %multiply_reduce_fusion.2 = f32[4096]{0:T(1024)S(1)} fusion(f32[4,128,4096]{1,2,0:T(8,128)} %fusion.72, f32[128]{0:T(128)S(1)} %compare_convert_fusion.3, pred[128,4096]{0,1:T(8,128)(4,1)S(1)} %compare_and_fusion.2, bf16[128,4,128]{0,2,1:T(8,128)(2,1)S(1)} %bitcast.71, bf16[4096,1024]{1,0:T(8,128)(2,1)} %get-tuple-element.300, s32[]{:T(128)S(6)} %select_n.79), kind=kOutput, calls=%fused_computation.5.clone.1 | convolution fusion | flops 551551488 | bytes 10633732 | tf_op jit(solution)/shard_map/while/body/eval_jaxpr/sub | solution.py:59
  265.3 8.6 %fusion.72 = f32[4,128,4096]{1,2,0:T(8,128)} fusion(pred[128,4096]{0,1:T(8,128)(4,1)S(1)} %compare_and_fusion.2, bf16[128,4,128]{0,2,1:T(8,128)(2,1)S(1)} %bitcast.70, bf16[4096,1024]{1,0:T(8,128)(2,1)} %get-tuple-element.300, s32[]{:T(128)S(6)} %select_n.79), kind=kOutput, calls=%fused_computation.2.clone.1 | convolution fusion | flops 545268736 | bytes 10616836 | tf_op jit(solution)/shard_map/while/body/eval_jaxpr/div | solution.py:61
  273.9 8.4 %multiply_reduce_fusion.2 = f32[4096]{0:T(1024)S(1)} fusion(f32[4,128,4096]{1,2,0:T(8,128)} %fusion.72, f32[128]{0:T(128)S(1)} %compare_convert_fusion.3, pred[128,4096]{0,1:T(8,128)(4,1)S(1)} %compare_and_fusion.2, bf16[128,4,128]{0,2,1:T(8,128)(2,1)S(1)} %bitcast.71, bf16[4096,1024]{1,0:T(8,128)(2,1)} %get-tuple-element.300, s32[]{:T(128)S(6)} %select_n.79), kind=kOutput, calls=%fused_computation.5.clone.1 | convolution fusion | flops 551551488 | bytes 10633732 | tf_op jit(solution)/shard_map/while/body/eval_jaxpr/sub | solution.py:59
  286.7 8.6 %fusion.72 = f32[4,128,4096]{1,2,0:T(8,128)} fusion(pred[128,4096]{0,1:T(8,128)(4,1)S(1)} %compare_and_fusion.2, bf16[128,4,128]{0,2,1:T(8,128)(2,1)S(1)} %bitcast.70, bf16[4096,1024]{1,0:T(8,128)(2,1)} %get-tuple-element.300, s32[]{:T(128)S(6)} %select_n.79), kind=kOutput, calls=%fused_computation.2.clone.1 | convolution fusion | flops 545268736 | bytes 10616836 | tf_op jit(solution)/shard_map/while/body/eval_jaxpr/div | solution.py:61
  295.3 8.4 %multiply_reduce_fusion.2 = f32[4096]{0:T(1024)S(1)} fusion(f32[4,128,4096]{1,2,0:T(8,128)} %fusion.72, f32[128]{0:T(128)S(1)} %compare_convert_fusion.3, pred[128,4096]{0,1:T(8,128)(4,1)S(1)} %compare_and_fusion.2, bf16[128,4,128]{0,2,1:T(8,128)(2,1)S(1)} %bitcast.71, bf16[4096,1024]{1,0:T(8,128)(2,1)} %get-tuple-element.300, s32[]{:T(128)S(6)} %select_n.79), kind=kOutput, calls=%fused_computation.5.clone.1 | convolution fusion | flops 551551488 | bytes 10633732 | tf_op jit(solution)/shard_map/while/body/eval_jaxpr/sub | solution.py:59
  305.3 14.0 %all-to-all-start.1 = ((f32[32,8,128]{2,1,0:T(8,128)}), f32[32,8,128]{2,1,0:T(8,128)S(1)}, u32[]{:S(2)}, u32[]{:S(2)}) async-start(f32[32,8,128]{2,1,0:T(8,128)} %bitcast.10), calls=%async_computation.1 | async-start | bytes 262144 | tf_op jit(solution)/shard_map/all_to_all | solution.py:15
  319.6 6.5 %multiply_convert_fusion = (bf16[128,1024]{1,0:T(8,128)(2,1)S(1)}, f32[128,1024]{1,0:T(8,128)S(1)}) fusion(f32[1024]{0:T(1024)S(1)} %copy-done.4, bf16[6144,1024]{1,0:T(8,128)(2,1)} %param.16, bf16[128,1024]{0,1:T(8,128)(2,1)S(1)} %bitcast.74, bf16[128,1024]{0,1:T(8,128)(2,1)S(1)} %bitcast.72, bf16[128,4096]{0,1:T(8,128)(2,1)S(1)} %get-tuple-element.318), kind=kOutput, calls=%fused_computation.42 | convolution fusion | flops 1616117760 | bytes 14946304 | tf_op jit(solution)/shard_map/dot_general | solution.py:71
  327.9 13.2 %fusion.46 = f32[6144,1024]{1,0:T(8,128)} fusion(bf16[128,1024]{1,0:T(8,128)(2,1)S(1)} %get-tuple-element.212, bf16[128,1024]{0,1:T(8,128)(2,1)S(1)} %bitcast.75, bf16[128,1024]{0,1:T(8,128)(2,1)S(1)} %bitcast.73, bf16[128,4096]{0,1:T(8,128)(2,1)S(1)} %get-tuple-element.318), kind=kOutput, calls=%fused_computation.40 | convolution fusion | flops 1615331328 | bytes 27000832 | tf_op jit(solution)/shard_map/dot_general | solution.py:93
  341.6 67.0 %psum.7 = f32[9224]{0:T(1024)S(1)} all-reduce(f32[9224]{0:T(1024)S(1)} %pad_maximum_fusion.3), channel_id=1, replica_groups=mesh['seq'=32,'batch'=4] {'seq','batch'}, use_global_device_ids=true, to_apply=%region_9.10 | all-reduce | flops 9224 | bytes 73792 | tf_op jit(solution)/shard_map/psum | solution.py:23
  410.8 178.8 %reduce-scatter.2.cloned.1.call-done = f32[48,1024]{1,0:T(8,128)} async-done(((f32[6144,1024]{1,0:T(8,128)}), f32[48,1024]{1,0:T(8,128)}) %reduce-scatter.2.cloned.1.call-update) | async-done | bytes 196624 | tf_op jit(solution)/shard_map/reduce_scatter | solution.py:92
  (71 shorter events, 47.0 us)
Async XLA Ops:
  7.2 320.0 %copy-start = (bf16[1024,8]{0,1:T(8,128)(2,1)S(1)}, bf16[1024,8]{0,1:T(8,128)(2,1)}, u32[]{:S(2)}) copy-start(bf16[1024,8]{0,1:T(8,128)(2,1)} %param.18) | copy-start | bytes 49156
  12.4 8.8 %copy-start.1 = (bf16[1,128,1024]{2,1,0:T(8,128)(2,1)S(1)}, bf16[1,128,1024]{2,1,0:T(8,128)(2,1)}, u32[]{:S(2)}) copy-start(bf16[1,128,1024]{2,1,0:T(8,128)(2,1)} %param.12) | copy-start | bytes 786436
  12.4 9.6 %copy-start.3 = (bf16[1,128,1024]{2,1,0:T(8,128)(2,1)S(1)}, bf16[1,128,1024]{2,1,0:T(8,128)(2,1)}, u32[]{:S(2)}) copy-start(bf16[1,128,1024]{2,1,0:T(8,128)(2,1)} %param.13) | copy-start | bytes 786436
  12.4 9.8 %copy-start.2 = (bf16[1,128,4096]{2,1,0:T(8,128)(2,1)S(1)}, bf16[1,128,4096]{2,1,0:T(8,128)(2,1)}, u32[]{:S(2)}) copy-start(bf16[1,128,4096]{2,1,0:T(8,128)(2,1)} %param.11) | copy-start | bytes 3145732
  12.4 10.5 %copy-start.5 = (s32[1,32]{1,0:T(1,128)S(1)}, s32[1,32]{1,0:T(1,128)}, u32[]{:S(2)}) copy-start(s32[1,32]{1,0:T(1,128)} %param.15) | copy-start | bytes 388
  12.4 122.2 %all-to-all-start = ((bf16[32,128,1024]{2,1,0:T(8,128)(2,1)}), bf16[32,128,1024]{2,1,0:T(8,128)(2,1)}, u32[]{:S(2)}, u32[]{:S(2)}) async-start(bf16[32,128,1024]{2,1,0:T(8,128)(2,1)} %stack.3), calls=%async_computation | async-start | bytes 16777216 | tf_op jit(solution)/shard_map/all_to_all | solution.py:37
  134.7 184.9 %copy-start.4 = (f32[1024]{0:T(1024)S(1)}, f32[1024]{0:T(1024)}, u32[]{:S(2)}) copy-start(f32[1024]{0:T(1024)} %param.17) | copy-start | bytes 12292
  305.3 21.9 %all-to-all-start.1 = ((f32[32,8,128]{2,1,0:T(8,128)}), f32[32,8,128]{2,1,0:T(8,128)S(1)}, u32[]{:S(2)}, u32[]{:S(2)}) async-start(f32[32,8,128]{2,1,0:T(8,128)} %bitcast.10), calls=%async_computation.1 | async-start | bytes 262144 | tf_op jit(solution)/shard_map/all_to_all | solution.py:15
  319.3 270.4 %reduce-scatter.2.cloned.1.call-start = ((), (), s32[]{:S(2)}) async-start(), calls=%async_computation.3 | async-start | bytes 25362432 | tf_op jit(solution)/shard_map/reduce_scatter | solution.py:92
  319.6 7.6 %copy-start.6 = (f32[8]{0:T(128)S(1)}, f32[8]{0:T(128)}, u32[]{:S(2)}) copy-start(f32[8]{0:T(128)} %param.19) | copy-start | bytes 100
Sparse Core Ops, SparseCore 0:
  341.2 248.4 reduce-scatter.1
